TPU v7x, 32 devices: a whole 2x2x4 slice. The times are simulated.
32 devices in a mesh: row: 4 (over z), col: 8 (over y, x, core).
Axes of the slice: x: 2, y: 2, z: 4, core: 2. Of those that a mesh axis runs over, the one named last changes fastest.
Arguments:
- hidden_in: bfloat16 [8192, 1536], P(('row', 'col')), may hold values from -6 to 6
- out_grad: bfloat16 [8192, 1536], P(('row', 'col')), may hold values from -6 to 6
- seq_lengths: int32 [4, 16], P('row'), may hold values from 1 to 1024, 2048 in all within a row
- norm1_gain: bfloat16 [1536], P(('row', 'col')), may hold values from 0.25 to 1.75
- q_weight: bfloat16 [1536, 1536], P('row', 'col'), may hold values from -0.15625 to 0.15625
- q_bias: bfloat16 [1536], P(('row', 'col')), may hold values from -3 to 3
- k_weight: bfloat16 [1536, 256], P('row', 'col'), may hold values from -0.15625 to 0.15625
- k_bias: bfloat16 [256], P(('row', 'col')), may hold values from -3 to 3
- v_weight: bfloat16 [1536, 256], P('row', 'col'), may hold values from -0.15625 to 0.15625
- v_bias: bfloat16 [256], P(('row', 'col')), may hold values from -3 to 3
- o_weight: bfloat16 [1536, 1536], P('row', 'col'), may hold values from -0.625 to 0.625
- norm2_gain: bfloat16 [1536], P(('row', 'col')), may hold values from 0.25 to 1.75
- gate_weight: bfloat16 [1536, 8960], P('row', 'col'), may hold values from -0.15625 to 0.15625
- up_weight: bfloat16 [1536, 8960], P('row', 'col'), may hold values from -0.15625 to 0.15625
- down_weight: bfloat16 [8960, 1536], P('col', 'row'), may hold values from -0.375 to 0.375
Outputs:
- layer_out: float32 [8192, 1536], P(('row', 'col'))
- input_grad: float32 [8192, 1536], P(('row', 'col'))
- norm1_gain_grad: float32 [1536], P(('row', 'col'))
- q_weight_grad: float32 [1536, 1536], P('row', 'col')
- q_bias_grad: float32 [1536], P(('row', 'col'))
- k_weight_grad: float32 [1536, 256], P('row', 'col')
- k_bias_grad: float32 [256], P(('row', 'col'))
- v_weight_grad: float32 [1536, 256], P('row', 'col')
- v_bias_grad: float32 [256], P(('row', 'col'))
- o_weight_grad: float32 [1536, 1536], P('row', 'col')
- norm2_gain_grad: float32 [1536], P(('row', 'col'))
- gate_weight_grad: float32 [1536, 8960], P('row', 'col')
- up_weight_grad: float32 [1536, 8960], P('row', 'col')
- down_weight_grad: float32 [8960, 1536], P('col', 'row')
Inputs may be any that keep to these rules, and one draw needn't show every extreme that they name: `seq_lengths`: row r lists the lengths of the 16 sequences packed in order into block r of 2048 tokens; they sum to 2048, and the longest is exactly 1024 in every row.
All inputs are finite; a program needn't handle non-finite values.
Results may differ from a plain program's by a relative error of at most 0.03.
Values may be sent and summed in bfloat16 or wider, within the bound.
A program may use at most 192 MiB of HBM per device.

v0:
```python
import math
import jax
import jax.numpy as jnp
from jax import lax
from jax.sharding import PartitionSpec as P

HQ = 12
KVH = 2
HD = 128
MAXLEN = 1024
EPSILON = 1e-06
ROPE_BASE = 1000000.0


def seq_starts(slots, lengths):
    bounds = jnp.cumsum(lengths)
    picked = jnp.where(bounds[None, :] <= slots[:, None], lengths[None, :], 0)
    return jnp.sum(picked, axis=1)


def rope_tables(positions, head_dim):
    steps_up = jnp.arange(head_dim // 2, dtype=jnp.float32)
    freqs = jnp.exp(-math.log(ROPE_BASE) * (2.0 * steps_up / head_dim))
    angles = positions.astype(jnp.float32)[:, None] * freqs[None, :]
    angles = jnp.concatenate([angles, angles], axis=1)
    return (jnp.cos(angles)[:, None, :], jnp.sin(angles)[:, None, :])


def rotate_pairs(values, cosines, sines):
    half_dim = values.shape[-1] // 2
    turned = jnp.concatenate([-values[..., half_dim:], values[..., :half_dim]], axis=-1)
    return values * cosines + turned * sines


def rotate_back(grads_in, cosines, sines):
    half_dim = grads_in.shape[-1] // 2
    moved = grads_in * sines
    return grads_in * cosines + jnp.concatenate(
        [moved[..., half_dim:], -moved[..., :half_dim]], axis=-1
    )


def rms_scale(values):
    return lax.rsqrt(jnp.mean(values * values, axis=-1, keepdims=True) + EPSILON)


def product(left, right):
    return jnp.dot(left, right, preferred_element_type=jnp.float32)


def contract_rows(left, right):
    return lax.dot_general(
        left, right, (((0,), (0,)), ((), ())), preferred_element_type=jnp.float32
    )


def contract_cols(left, right):
    return lax.dot_general(
        left, right, (((1,), (1,)), ((), ())), preferred_element_type=jnp.float32
    )


def rounded_wide(values):
    return lax.optimization_barrier(values.astype(jnp.bfloat16)).astype(jnp.float32)


def assemble(stacked, row_parts, col_parts):
    height, width = (stacked.shape[1], stacked.shape[2])
    grid = stacked.reshape(row_parts, col_parts, height, width).transpose(0, 2, 1, 3)
    return grid.reshape(row_parts * height, col_parts * width)


def split_blocks(full, row_parts, col_parts):
    height = full.shape[0] // row_parts
    width = full.shape[1] // col_parts
    grid = full.reshape(row_parts, height, col_parts, width).transpose(0, 2, 1, 3)
    return grid.reshape(row_parts * col_parts, height, width)


def unpack_attention(stacked, row_parts, col_parts):
    matrices = tuple((assemble(member, row_parts, col_parts) for member in stacked[:4]))
    return matrices + tuple(stacked[4:])


def masked_scores(query_heads, keys_window, visible, score_scale):
    scores = jnp.einsum(
        "tkgd,skd->kgts", query_heads, keys_window, preferred_element_type=jnp.float32
    )
    return jnp.where(visible, scores * score_scale, -jnp.inf)


def shards(
    hidden_in,
    out_grad,
    seq_lengths,
    norm1_gain,
    q_weight,
    q_bias,
    k_weight,
    k_bias,
    v_weight,
    v_bias,
    o_weight,
    norm2_gain,
    gate_weight,
    up_weight,
    down_weight,
):
    row_parts = lax.axis_size("row")
    col_parts = lax.axis_size("col")
    col_place = lax.axis_index("col")
    stacked = (
        lax.all_gather(q_weight[None], ("row", "col"), axis=0, tiled=True),
        lax.all_gather(k_weight[None], ("row", "col"), axis=0, tiled=True),
        lax.all_gather(v_weight[None], ("row", "col"), axis=0, tiled=True),
        lax.all_gather(o_weight[None], ("row", "col"), axis=0, tiled=True),
        lax.all_gather(q_bias, ("row", "col"), axis=0, tiled=True),
        lax.all_gather(k_bias, ("row", "col"), axis=0, tiled=True),
        lax.all_gather(v_bias, ("row", "col"), axis=0, tiled=True),
        lax.all_gather(norm1_gain, ("row", "col"), axis=0, tiled=True),
        lax.all_gather(norm2_gain, ("row", "col"), axis=0, tiled=True),
    )
    attention = unpack_attention(stacked, row_parts, col_parts)
    gate_block, up_block, down_block = (
        lax.all_gather(gate_weight, "row", axis=0, tiled=True),
        lax.all_gather(up_weight, "row", axis=0, tiled=True),
        lax.all_gather(down_weight, "row", axis=1, tiled=True),
    )
    (
        query_matrix,
        key_matrix,
        value_matrix,
        output_matrix,
        query_offset,
        key_offset,
        value_offset,
        first_gain,
        second_gain,
    ) = attention
    own_rows = hidden_in.shape[0]
    row_tokens = own_rows * col_parts
    lengths = seq_lengths[0]
    query_slots = col_place * own_rows + jnp.arange(own_rows, dtype=jnp.int32)
    query_starts = seq_starts(query_slots, lengths)
    cosines, sines = rope_tables(query_slots - query_starts, HD)
    group_size = HQ // KVH
    score_scale = 1.0 / math.sqrt(HD)
    inputs_wide = hidden_in.astype(jnp.float32)
    first_rms = rms_scale(inputs_wide)
    first_unit = inputs_wide * first_rms
    first_normed = (first_unit * first_gain.astype(jnp.float32)).astype(jnp.bfloat16)
    query_base = product(first_normed, query_matrix) + query_offset.astype(jnp.float32)
    key_base = product(first_normed, key_matrix) + key_offset.astype(jnp.float32)
    value_own = (product(first_normed, value_matrix) + value_offset.astype(jnp.float32)).astype(
        jnp.bfloat16
    )
    queries = rotate_pairs(query_base.reshape(own_rows, HQ, HD), cosines, sines).astype(
        jnp.bfloat16
    )
    keys_own = rotate_pairs(key_base.reshape(own_rows, KVH, HD), cosines, sines).astype(
        jnp.bfloat16
    )
    keys_all, values_all = (
        lax.all_gather(keys_own.reshape(own_rows, KVH * HD), "col", axis=0, tiled=True),
        lax.all_gather(value_own, "col", axis=0, tiled=True),
    )
    window = min(own_rows + MAXLEN, row_tokens)
    window_start = jnp.clip(col_place * own_rows - MAXLEN, 0, row_tokens - window)
    key_slots = window_start + jnp.arange(window, dtype=jnp.int32)
    key_starts = seq_starts(key_slots, lengths)
    visible = (query_starts[:, None] == key_starts[None, :]) & (
        key_slots[None, :] <= query_slots[:, None]
    )
    keys_window = lax.dynamic_slice_in_dim(keys_all, window_start, window, 0).reshape(
        window, KVH, HD
    )
    values_window = lax.dynamic_slice_in_dim(values_all, window_start, window, 0).reshape(
        window, KVH, HD
    )
    query_heads = queries.reshape(own_rows, KVH, group_size, HD)
    scores = masked_scores(query_heads, keys_window, visible, score_scale)
    peak = jnp.max(scores, axis=-1, keepdims=True)
    expanded = jnp.exp(scores - peak)
    totals = jnp.sum(expanded, axis=-1, keepdims=True)
    probs = expanded / totals
    log_total = peak + jnp.log(totals)
    mixed = jnp.einsum(
        "kgts,skd->tkgd",
        probs.astype(jnp.bfloat16),
        values_window,
        preferred_element_type=jnp.float32,
    )
    mixed = mixed.reshape(own_rows, HQ * HD).astype(jnp.bfloat16)
    residual = inputs_wide + product(mixed, output_matrix)
    second_rms = rms_scale(residual)
    second_unit = residual * second_rms
    second_normed = (second_unit * second_gain.astype(jnp.float32)).astype(jnp.bfloat16)
    normed_rows = lax.all_gather(second_normed, "col", axis=0, tiled=True)
    gate_act = product(normed_rows, gate_block)
    up_act = product(normed_rows, up_block)
    sigmoid_gate = jax.nn.sigmoid(gate_act)
    silu_gate = gate_act * sigmoid_gate
    hidden = (silu_gate * up_act).astype(jnp.bfloat16)
    branch_out = lax.psum_scatter(
        product(hidden, down_block), "col", scatter_dimension=0, tiled=True
    )
    layer_out = residual + branch_out
    stacked_again = (
        lax.all_gather(q_weight[None], ("row", "col"), axis=0, tiled=True),
        lax.all_gather(k_weight[None], ("row", "col"), axis=0, tiled=True),
        lax.all_gather(v_weight[None], ("row", "col"), axis=0, tiled=True),
        lax.all_gather(o_weight[None], ("row", "col"), axis=0, tiled=True),
        lax.all_gather(q_bias, ("row", "col"), axis=0, tiled=True),
        lax.all_gather(k_bias, ("row", "col"), axis=0, tiled=True),
        lax.all_gather(v_bias, ("row", "col"), axis=0, tiled=True),
        lax.all_gather(norm1_gain, ("row", "col"), axis=0, tiled=True),
        lax.all_gather(norm2_gain, ("row", "col"), axis=0, tiled=True),
    )
    (
        query_matrix,
        key_matrix,
        value_matrix,
        output_matrix,
        query_offset,
        key_offset,
        value_offset,
        first_gain,
        second_gain,
    ) = unpack_attention(stacked_again, row_parts, col_parts)
    gate_block, up_block, down_block = (
        lax.all_gather(gate_weight, "row", axis=0, tiled=True),
        lax.all_gather(up_weight, "row", axis=0, tiled=True),
        lax.all_gather(down_weight, "row", axis=1, tiled=True),
    )
    out_rows = lax.all_gather(out_grad, "col", axis=0, tiled=True)
    hidden_grad = contract_cols(out_rows, down_block)
    down_grad = contract_rows(hidden, out_rows)
    up_grad_act = (hidden_grad * silu_gate).astype(jnp.bfloat16)
    gate_grad_act = (
        hidden_grad * up_act * sigmoid_gate * (1.0 + gate_act * (1.0 - sigmoid_gate))
    ).astype(jnp.bfloat16)
    gate_grad = contract_rows(normed_rows, gate_grad_act)
    up_grad = contract_rows(normed_rows, up_grad_act)
    normed_grad = lax.psum_scatter(
        contract_cols(gate_grad_act, gate_block) + contract_cols(up_grad_act, up_block),
        "col",
        scatter_dimension=0,
        tiled=True,
    )
    second_gain_grad = jnp.sum(normed_grad * second_unit, axis=0)
    unit_grad = normed_grad * second_gain.astype(jnp.float32)
    residual_grad = out_grad.astype(jnp.float32) + second_rms * (
        unit_grad - second_unit * jnp.mean(unit_grad * second_unit, axis=-1, keepdims=True)
    )
    attended_grad = residual_grad.astype(jnp.bfloat16)
    mixed_grad = contract_cols(attended_grad, output_matrix).astype(jnp.bfloat16)
    grad_heads = mixed_grad.reshape(own_rows, KVH, group_size, HD)
    scores = masked_scores(query_heads, keys_window, visible, score_scale)
    probs = jnp.exp(scores - log_total)
    prob_grad = jnp.einsum(
        "tkgd,skd->kgts", grad_heads, values_window, preferred_element_type=jnp.float32
    )
    value_part = jnp.einsum(
        "kgts,tkgd->skd", probs.astype(jnp.bfloat16), grad_heads, preferred_element_type=jnp.float32
    )
    score_grad = (probs * (prob_grad - jnp.sum(probs * prob_grad, axis=-1, keepdims=True))).astype(
        jnp.bfloat16
    )
    query_grad = (
        jnp.einsum("kgts,skd->tkgd", score_grad, keys_window, preferred_element_type=jnp.float32)
        * score_scale
    )
    key_part = (
        jnp.einsum("kgts,tkgd->skd", score_grad, query_heads, preferred_element_type=jnp.float32)
        * score_scale
    )
    empty_rows = jnp.zeros((row_tokens, KVH * HD), jnp.float32)
    key_rows = lax.dynamic_update_slice_in_dim(
        empty_rows, key_part.reshape(window, KVH * HD), window_start, 0
    )
    value_rows = lax.dynamic_update_slice_in_dim(
        empty_rows, value_part.reshape(window, KVH * HD), window_start, 0
    )
    key_grad, value_grad = (
        lax.psum_scatter(key_rows, "col", scatter_dimension=0, tiled=True),
        lax.psum_scatter(value_rows, "col", scatter_dimension=0, tiled=True),
    )
    query_wide = rounded_wide(query_grad.reshape(own_rows, HQ, HD))
    query_base_grad = (
        rotate_back(query_wide, cosines, sines).reshape(own_rows, HQ * HD).astype(jnp.bfloat16)
    )
    key_wide = rounded_wide(key_grad.reshape(own_rows, KVH, HD))
    key_base_grad = (
        rotate_back(key_wide, cosines, sines).reshape(own_rows, KVH * HD).astype(jnp.bfloat16)
    )
    value_base_grad = value_grad.astype(jnp.bfloat16)
    query_b_grad = jnp.sum(query_base_grad.astype(jnp.float32), axis=0)
    key_b_grad = jnp.sum(key_base_grad.astype(jnp.float32), axis=0)
    value_b_grad = jnp.sum(value_base_grad.astype(jnp.float32), axis=0)
    first_normed_grad = (
        contract_cols(query_base_grad, query_matrix)
        + contract_cols(key_base_grad, key_matrix)
        + contract_cols(value_base_grad, value_matrix)
    )
    first_gain_grad = jnp.sum(first_normed_grad * first_unit, axis=0)
    first_unit_grad = first_normed_grad * first_gain.astype(jnp.float32)
    input_grad = residual_grad + first_rms * (
        first_unit_grad
        - first_unit * jnp.mean(first_unit_grad * first_unit, axis=-1, keepdims=True)
    )
    attn_grads = (
        lax.psum_scatter(
            split_blocks(contract_rows(first_normed, query_base_grad), row_parts, col_parts),
            ("row", "col"),
            scatter_dimension=0,
            tiled=True,
        ),
        lax.psum_scatter(
            split_blocks(contract_rows(first_normed, key_base_grad), row_parts, col_parts),
            ("row", "col"),
            scatter_dimension=0,
            tiled=True,
        ),
        lax.psum_scatter(
            split_blocks(contract_rows(first_normed, value_base_grad), row_parts, col_parts),
            ("row", "col"),
            scatter_dimension=0,
            tiled=True,
        ),
        lax.psum_scatter(
            split_blocks(contract_rows(mixed, attended_grad), row_parts, col_parts),
            ("row", "col"),
            scatter_dimension=0,
            tiled=True,
        ),
        lax.psum_scatter(query_b_grad, ("row", "col"), scatter_dimension=0, tiled=True),
        lax.psum_scatter(key_b_grad, ("row", "col"), scatter_dimension=0, tiled=True),
        lax.psum_scatter(value_b_grad, ("row", "col"), scatter_dimension=0, tiled=True),
        lax.psum_scatter(first_gain_grad, ("row", "col"), scatter_dimension=0, tiled=True),
        lax.psum_scatter(second_gain_grad, ("row", "col"), scatter_dimension=0, tiled=True),
    )
    query_w_out = attn_grads[0][0]
    key_w_out = attn_grads[1][0]
    value_w_out = attn_grads[2][0]
    output_w_out = attn_grads[3][0]
    small_out = attn_grads[4:9]
    mlp_grads = (
        lax.psum_scatter(gate_grad, "row", scatter_dimension=0, tiled=True),
        lax.psum_scatter(up_grad, "row", scatter_dimension=0, tiled=True),
        lax.psum_scatter(down_grad, "row", scatter_dimension=1, tiled=True),
    )
    return (
        layer_out,
        input_grad,
        small_out[3],
        query_w_out,
        small_out[0],
        key_w_out,
        small_out[1],
        value_w_out,
        small_out[2],
        output_w_out,
        small_out[4],
        mlp_grads[0],
        mlp_grads[1],
        mlp_grads[2],
    )


def solution(mesh):
    in_specs = (
        P(("row", "col"), None),
        P(("row", "col"), None),
        P("row", None),
        P(("row", "col")),
        P("row", "col"),
        P(("row", "col")),
        P("row", "col"),
        P(("row", "col")),
        P("row", "col"),
        P(("row", "col")),
        P("row", "col"),
        P(("row", "col")),
        P("row", "col"),
        P("row", "col"),
        P("col", "row"),
    )
    out_specs = (
        P(("row", "col"), None),
        P(("row", "col"), None),
        P(("row", "col")),
        P("row", "col"),
        P(("row", "col")),
        P("row", "col"),
        P(("row", "col")),
        P("row", "col"),
        P(("row", "col")),
        P("row", "col"),
        P(("row", "col")),
        P("row", "col"),
        P("row", "col"),
        P("col", "row"),
    )
    return jax.shard_map(shards, mesh=mesh, in_specs=in_specs, out_specs=out_specs, check_vma=False)
```

profile of v0, /device:TPU:0, one launch (start us, length us, event | category | flops | bytes accessed | tf_op | source)
XLA Modules:
  0.0 1829.9 jit_solution(13234642449965689146)
XLA Ops:
  11.6 42.2 %all-reduce.11 = (bf16[256]{0:T(256)(128)(2,1)S(1)}, bf16[1536]{0:T(1024)(128)(2,1)S(1)}, bf16[256]{0:T(256)(128)(2,1)S(1)}, bf16[1536]{0:T(1024)(128)(2,1)S(1)}, bf16[1536]{0:T(1024)(128)(2,1)S(1)}) all-reduce(bf16[256]{0:T(256)(128)(2,1)S(1)} %dynamic-update-slice.1, ...), channel_id=1, replica_groups=mesh['row'=4,'col'=8] {'row','col'}, use_global_device_ids=true, to_apply=%add.1 | all-reduce | flops 5120 | bytes 20480
  55.2 42.7 %all-gather = bf16[12288,32]{0,1:T(8,128)(2,1)S(1)} all-gather(bf16[384,32]{0,1:T(8,128)(2,1)} %param.23), channel_id=2, replica_groups=mesh['row'=4,'col'=8] {'row','col'}, dimensions={0}, use_global_device_ids=true | all-gather | bytes 811008 | tf_op jit(solution)/shard_map/all_gather | solution.py:115
  100.5 39.0 %all-gather.1 = bf16[12288,32]{0,1:T(8,128)(2,1)S(1)} all-gather(bf16[384,32]{0,1:T(8,128)(2,1)S(1)} %copy-done.32), channel_id=3, replica_groups=mesh['row'=4,'col'=8] {'row','col'}, dimensions={0}, use_global_device_ids=true | all-gather | bytes 811008 | tf_op jit(solution)/shard_map/all_gather | solution.py:114
  148.0 15.2 all-gather.16.cloned.1.call-done
  164.7 65.0 %all-gather.28.cloned.1.call-done = bf16[12288,192]{0,1:T(8,128)(2,1)} async-done(((bf16[384,192]{0,1:T(8,128)(2,1)}), bf16[12288,192]{0,1:T(8,128)(2,1)}) %all-gather.28.cloned.1.call-update) | async-done | bytes 4718608 | tf_op jit(solution)/shard_map/all_gather | solution.py:113
  243.6 50.6 %all-gather.30.cloned.1.call-done = bf16[12288,192]{0,1:T(8,128)(2,1)} async-done(((bf16[384,192]{0,1:T(8,128)(2,1)}), bf16[12288,192]{0,1:T(8,128)(2,1)}) %all-gather.30.cloned.1.call-update) | async-done | bytes 4718608 | tf_op jit(solution)/shard_map/all_gather | solution.py:116
  301.3 16.6 fusion.46
  337.8 24.1 %all-gather.20.cloned.1.call-done = bf16[1536,1120]{0,1:T(8,128)(2,1)} async-done(((bf16[384,1120]{0,1:T(8,128)(2,1)}), bf16[1536,1120]{0,1:T(8,128)(2,1)}) %all-gather.20.cloned.1.call-update) | async-done | bytes 3440656 | tf_op jit(solution)/shard_map/all_gather | solution.py:125
  361.9 46.3 %all-gather.18.cloned.1.call-done = bf16[2048,1536]{1,0:T(8,128)(2,1)} async-done(((bf16[256,1536]{1,0:T(8,128)(2,1)}), bf16[2048,1536]{1,0:T(8,128)(2,1)}) %all-gather.18.cloned.1.call-update) | async-done | bytes 6291472 | tf_op jit(solution)/shard_map/all_gather | solution.py:198
  421.1 56.8 %all-gather.22.cloned.1.call-done = bf16[1536,1120]{0,1:T(8,128)(2,1)} async-done(((bf16[384,1120]{0,1:T(8,128)(2,1)}), bf16[1536,1120]{0,1:T(8,128)(2,1)}) %all-gather.22.cloned.1.call-update) | async-done | bytes 3440656 | tf_op jit(solution)/shard_map/all_gather | solution.py:126
  490.8 55.4 %all-gather.24.cloned.1.call-done = bf16[1120,1536]{1,0:T(8,128)(2,1)} async-done(((bf16[1120,384]{1,0:T(8,128)(2,1)}), bf16[1120,1536]{1,0:T(8,128)(2,1)}) %all-gather.24.cloned.1.call-update) | async-done | bytes 3440656 | tf_op jit(solution)/shard_map/all_gather | solution.py:127
  546.2 45.9 %all-gather.26.cloned.1.call-done = bf16[2048,1536]{1,0:T(8,128)(2,1)} async-done(((bf16[256,1536]{1,0:T(8,128)(2,1)}), bf16[2048,1536]{1,0:T(8,128)(2,1)}) %all-gather.26.cloned.1.call-update) | async-done | bytes 6291472 | tf_op jit(solution)/shard_map/all_gather | solution.py:235
  592.1 20.8 %multiply_convert_fusion = (bf16[2048,1120]{0,1:T(8,128)(2,1)}, bf16[2048,1120]{0,1:T(8,128)(2,1)}, bf16[2048,1120]{0,1:T(8,128)(2,1)}) fusion(f32[2048,1120]{0,1:T(8,128)} %fusion.47, f32[2048,1120]{0,1:T(8,128)} %fusion.48, bf16[2048,1536]{1,0:T(8,128)(2,1)} %all-gather.26.cloned.1.call-done, bf16[1120,1536]{1,0:T(8,128)(2,1)} %all-gather.24.cloned.1.call-done), kind=kOutput, calls=%fused_computation.11 | convolution fusion | flops 7080837120 | bytes 41844736 | tf_op jit(solution)/shard_map/dot_general | solution.py:58
  640.4 15.2 fusion.49
  655.9 76.9 %reduce-scatter.14.cloned.1.call-done = f32[256,1536]{1,0:T(8,128)} async-done(((f32[2048,1536]{1,0:T(8,128)}), f32[256,1536]{1,0:T(8,128)}) %reduce-scatter.14.cloned.1.call-update) | async-done | bytes 1572880 | tf_op jit(solution)/shard_map/reduce_scatter | solution.py:244
  734.6 94.0 %reduce-scatter.12.cloned.1.call-done = f32[256,1536]{1,0:T(8,128)} async-done(((f32[2048,1536]{1,0:T(8,128)}), f32[256,1536]{1,0:T(8,128)}) %reduce-scatter.12.cloned.1.call-update) | async-done | bytes 1572880 | tf_op jit(solution)/shard_map/reduce_scatter | solution.py:204
  993.0 44.7 %all-reduce.10 = (f32[1536]{0:T(1024)S(1)}, f32[1536]{0:T(1024)S(1)}, f32[256]{0:T(256)S(1)}, f32[256]{0:T(256)S(1)}, f32[1536]{0:T(1024)S(1)}) all-reduce(f32[1536]{0:T(1024)S(1)} %copy-done.31, f32[1536]{0:T(1024)S(1)} %bitcast.257, f32[256]{0:T(256)S(1)} %bitcast.261, ...), channel_id=10, replica_groups=mesh['row'=4,'col'=8] {'row','col'}, use_global_device_ids=true, to_apply=%region_15.16.clone | all-reduce | flops 5120 | bytes 40960
  1043.5 42.1 %reduce-scatter.28.cloned.1.call-done = f32[384,1120]{0,1:T(8,128)} async-done(((f32[1536,1120]{0,1:T(8,128)}), f32[384,1120]{0,1:T(8,128)}) %reduce-scatter.28.cloned.1.call-update) | async-done | bytes 1720336 | tf_op jit(solution)/shard_map/reduce_scatter | solution.py:348
  1085.6 123.6 %reduce-scatter.30.cloned.1.call-done = f32[384,1120]{0,1:T(8,128)} async-done(((f32[1536,1120]{0,1:T(8,128)}), f32[384,1120]{0,1:T(8,128)}) %reduce-scatter.30.cloned.1.call-update) | async-done | bytes 1720336 | tf_op jit(solution)/shard_map/reduce_scatter | solution.py:349
  1209.2 123.6 %reduce-scatter.32.cloned.1.call-done = f32[1120,384]{1,0:T(8,128)} async-done(((f32[1120,1536]{1,0:T(8,128)}), f32[1120,384]{1,0:T(8,128)}) %reduce-scatter.32.cloned.1.call-update) | async-done | bytes 1720336 | tf_op jit(solution)/shard_map/reduce_scatter | solution.py:350
  1332.8 104.1 %reduce-scatter.22.cloned.1.call-done = f32[1,384,32]{1,2,0:T(8,128)} async-done(((f32[32,384,32]{1,2,0:T(8,128)}), f32[1,384,32]{1,2,0:T(8,128)}) %reduce-scatter.22.cloned.1.call-update) | async-done | bytes 49168 | tf_op jit(solution)/shard_map/reduce_scatter | solution.py:318
  1437.0 102.6 %reduce-scatter.24.cloned.1.call-done = f32[1,384,32]{1,2,0:T(8,128)} async-done(((f32[32,384,32]{1,2,0:T(8,128)}), f32[1,384,32]{1,2,0:T(8,128)}) %reduce-scatter.24.cloned.1.call-update) | async-done | bytes 49168 | tf_op jit(solution)/shard_map/reduce_scatter | solution.py:324
  1539.6 141.7 %reduce-scatter.26.cloned.1.call-done = f32[1,384,192]{1,2,0:T(8,128)} async-done(((f32[32,384,192]{1,2,0:T(8,128)}), f32[1,384,192]{1,2,0:T(8,128)}) %reduce-scatter.26.cloned.1.call-update) | async-done | bytes 294928 | tf_op jit(solution)/shard_map/reduce_scatter | solution.py:330
  1681.3 141.5 %reduce-scatter.20.cloned.1.call-done = f32[1,384,192]{1,2,0:T(8,128)} async-done(((f32[32,384,192]{1,2,0:T(8,128)}), f32[1,384,192]{1,2,0:T(8,128)}) %reduce-scatter.20.cloned.1.call-update) | async-done | bytes 294928 | tf_op jit(solution)/shard_map/reduce_scatter | solution.py:312
  (244 shorter events, 283.9 us)
Async XLA Ops:
  7.2 138.5 %all-gather.14.cloned.1.call-start = ((), (), s32[]{:S(2)}) async-start(), calls=%async_computation.11 | async-start | bytes 1179648 | tf_op jit(solution)/shard_map/all_gather | solution.py:165
  53.8 181.9 %copy-start.28 = (f32[1536]{0:T(1024)}, f32[1536]{0:T(1024)S(1)}, u32[]{:S(2)}) copy-start(f32[1536]{0:T(1024)S(1)} %convert_element_type.134) | copy-start | bytes 18436
  55.2 180.6 %copy-start.33 = (f32[256]{0:T(256)}, f32[256]{0:T(256)S(1)}, u32[]{:S(2)}) copy-start(f32[256]{0:T(256)S(1)} %add_rsqrt_fusion.1) | copy-start | bytes 3076
  100.5 62.8 %all-gather.16.cloned.1.call-start = ((), (), s32[]{:S(2)}) async-start(), calls=%async_computation.12 | async-start | bytes 1179648 | tf_op jit(solution)/shard_map/all_gather | solution.py:164
  141.0 159.3 %copy-start.12 = (f32[256,128]{0,1:T(8,128)}, f32[256,128]{0,1:T(8,128)S(1)}, u32[]{:S(2)}) copy-start(f32[256,128]{0,1:T(8,128)S(1)} %get-tuple-element.47) | copy-start | bytes 393220
  142.3 87.4 %all-gather.28.cloned.1.call-start = ((), (), s32[]{:S(2)}) async-start(), calls=%async_computation.29 | async-start | bytes 4866048 | tf_op jit(solution)/shard_map/all_gather | solution.py:113
  143.0 151.2 %all-gather.30.cloned.1.call-start = ((), (), s32[]{:S(2)}) async-start(), calls=%async_computation.30 | async-start | bytes 4866048 | tf_op jit(solution)/shard_map/all_gather | solution.py:116
  143.6 218.3 %all-gather.20.cloned.1.call-start = ((), (), s32[]{:S(2)}) async-start(), calls=%async_computation.14 | async-start | bytes 4300800 | tf_op jit(solution)/shard_map/all_gather | solution.py:125
  144.2 264.0 %all-gather.18.cloned.1.call-start = ((), (), s32[]{:S(2)}) async-start(), calls=%async_computation.13 | async-start | bytes 7077888 | tf_op jit(solution)/shard_map/all_gather | solution.py:198
  335.5 142.4 %all-gather.22.cloned.1.call-start = ((), (), s32[]{:S(2)}) async-start(), calls=%async_computation.15 | async-start | bytes 4300800 | tf_op jit(solution)/shard_map/all_gather | solution.py:126
  336.3 209.9 %all-gather.24.cloned.1.call-start = ((), (), s32[]{:S(2)}) async-start(), calls=%async_computation.16 | async-start | bytes 4300800 | tf_op jit(solution)/shard_map/all_gather | solution.py:127
  337.0 255.0 %all-gather.26.cloned.1.call-start = ((), (), s32[]{:S(2)}) async-start(), calls=%async_computation.18 | async-start | bytes 7077888 | tf_op jit(solution)/shard_map/all_gather | solution.py:235
  337.8 395.0 %reduce-scatter.14.cloned.1.call-start = ((), (), s32[]{:S(2)}) async-start(), calls=%async_computation.19 | async-start | bytes 14155776 | tf_op jit(solution)/shard_map/reduce_scatter | solution.py:244
  640.3 188.3 %reduce-scatter.12.cloned.1.call-start = ((), (), s32[]{:S(2)}) async-start(), calls=%async_computation.17 | async-start | bytes 14155776 | tf_op jit(solution)/shard_map/reduce_scatter | solution.py:204
  655.6 173.0 %copy-start.17 = (bf16[256,1536]{1,0:T(8,128)(2,1)S(1)}, bf16[256,1536]{1,0:T(8,128)(2,1)}, u32[]{:S(2)}) copy-start(bf16[256,1536]{1,0:T(8,128)(2,1)} %param.16) | copy-start | bytes 2359300
  655.6 291.5 %reduce-scatter.16.cloned.1.call-start = ((), (), s32[]{:S(2)}) async-start(), calls=%async_computation.20 | async-start | bytes 2359296 | tf_op jit(solution)/shard_map/reduce_scatter | solution.py:285
  875.8 85.7 %reduce-scatter.18.cloned.1.call-start = ((), (), s32[]{:S(2)}) async-start(), calls=%async_computation.21 | async-start | bytes 2359296 | tf_op jit(solution)/shard_map/reduce_scatter | solution.py:286
  895.2 190.4 %reduce-scatter.28.cloned.1.call-start = ((), (), s32[]{:S(2)}) async-start(), calls=%async_computation.26 | async-start | bytes 8601600 | tf_op jit(solution)/shard_map/reduce_scatter | solution.py:348
  908.2 301.0 %reduce-scatter.30.cloned.1.call-start = ((), (), s32[]{:S(2)}) async-start(), calls=%async_computation.27 | async-start | bytes 8601600 | tf_op jit(solution)/shard_map/reduce_scatter | solution.py:349
  921.2 411.6 %reduce-scatter.32.cloned.1.call-start = ((), (), s32[]{:S(2)}) async-start(), calls=%async_computation.28 | async-start | bytes 8601600 | tf_op jit(solution)/shard_map/reduce_scatter | solution.py:350
  933.9 503.1 %reduce-scatter.22.cloned.1.call-start = ((), (), s32[]{:S(2)}) async-start(), calls=%async_computation.23 | async-start | bytes 1622016 | tf_op jit(solution)/shard_map/reduce_scatter | solution.py:318
  968.8 570.8 %reduce-scatter.24.cloned.1.call-start = ((), (), s32[]{:S(2)}) async-start(), calls=%async_computation.24 | async-start | bytes 1622016 | tf_op jit(solution)/shard_map/reduce_scatter | solution.py:324
  976.9 704.4 %reduce-scatter.26.cloned.1.call-start = ((), (), s32[]{:S(2)}) async-start(), calls=%async_computation.25 | async-start | bytes 9732096 | tf_op jit(solution)/shard_map/reduce_scatter | solution.py:330
  986.0 836.8 %reduce-scatter.20.cloned.1.call-start = ((), (), s32[]{:S(2)}) async-start(), calls=%async_computation.22 | async-start | bytes 9732096 | tf_op jit(solution)/shard_map/reduce_scatter | solution.py:312
  (42 other events, 638.6 us)
Sparse Core Ops, SparseCore 0:
  100.6 21.2 all-gather.13
  142.4 20.8 all-gather.15
  166.1 63.5 all-gather.27
  232.3 61.8 all-gather.29
  295.6 66.2 all-gather.19
  364.2 43.9 all-gather.17
  409.8 68.0 all-gather.21
  479.5 66.6 all-gather.23
  548.1 43.9 all-gather.25
  640.4 92.2 reduce-scatter.13
  736.3 92.2 reduce-scatter.11
  875.9 41.1 reduce-scatter.15
  920.3 41.0 reduce-scatter.17
  964.2 121.3 reduce-scatter.27
  1088.3 120.8 reduce-scatter.29
  1212.0 120.8 reduce-scatter.31
  1338.5 98.4 reduce-scatter.21
  1442.6 96.8 reduce-scatter.23
  1546.1 135.2 reduce-scatter.25
  1687.6 135.1 reduce-scatter.19
where the time goes:
time: 1840 us; the launch traced here: 1830 us
  waiting for transfers between devices  1320 us (72%)
  matrix products  215 us (12%)
  blocking collectives  169 us (9%)
  local copies, waits for them, and re-layouts  71.5 us (4%)
  other arithmetic  34.8 us (2%)
    reduce_scatter x1, waiting for transfers between devices, shards(): lax.psum_scatter(split_blocks(contract_rows(mixed, attended_grad), row_pa...  142 us
    reduce_scatter x1, waiting for transfers between devices, shards(): lax.psum_scatter(split_blocks(contract_rows(first_normed, query_base_grad...  142 us
    reduce_scatter x1, waiting for transfers between devices, shards(): lax.psum_scatter(down_grad, 'row', scatter_dimension=1, tiled=True)  124 us
    reduce_scatter x1, waiting for transfers between devices, shards(): lax.psum_scatter(up_grad, 'row', scatter_dimension=0, tiled=True)  124 us
    reduce_scatter x1, waiting for transfers between devices, shards(): lax.psum_scatter(split_blocks(contract_rows(first_normed, key_base_grad),...  104 us
    reduce_scatter x1, waiting for transfers between devices, shards(): lax.psum_scatter(split_blocks(contract_rows(first_normed, value_base_grad...  103 us
    reduce_scatter x1, waiting for transfers between devices, shards(): lax.psum_scatter(product(hidden, down_block), 'col', scatter_dimension=0,...  94 us
    unnamed x2, blocking collectives  86.9 us
  transfers between devices with their start and end apart: 20, of which 18 were waited for; matrix products, arithmetic and copies ran while one was open for 12% of the time, Pallas kernels for 0%

commit v1 on v0

--- a/solution.py
+++ b/solution.py
@@ -10,6 +10,19 @@
 MAXLEN = 1024
 EPSILON = 1e-06
 ROPE_BASE = 1000000.0
+
+
+def gather_around(value, axis, dim):
+    size, index, width = (lax.axis_size(axis), lax.axis_index(axis), value.shape[dim])
+    right = [(i, (i + 1) % size) for i in range(size)]
+    filled = jnp.zeros((*value.shape[:dim], size * width, *value.shape[dim + 1 :]), value.dtype)
+    block = value
+    for lap in range(size):
+        source = (index - lap) % size
+        filled = lax.dynamic_update_slice_in_dim(filled, block, source * width, axis=dim)
+        if lap < size - 1:
+            block = lax.ppermute(block, axis, right)
+    return filled
 
 
 def seq_starts(slots, lengths):
@@ -124,7 +137,7 @@
     gate_block, up_block, down_block = (
         lax.all_gather(gate_weight, "row", axis=0, tiled=True),
         lax.all_gather(up_weight, "row", axis=0, tiled=True),
-        lax.all_gather(down_weight, "row", axis=1, tiled=True),
+        gather_around(down_weight, "row", 1),
     )
     (
         query_matrix,

time: 1840 us -> 1840 us (level)
    reduce_scatter x1, waiting for transfers between devices: 76.9 us -> 10.5 us  [shards(): lax.psum_scatter(contract_cols(gate_grad_act, gate_block) + contract_cols...]
    ppermute x0 -> x3, waiting for transfers between devices: none -> 62.4 us  [gather_around(): block = lax.ppermute(block, axis, right)]
  transfers between devices with their start and end apart: 20 -> 23, of which waited for: 18 -> 21; matrix products, arithmetic and copies ran while one was open for 12% -> 11% of each run, Pallas kernels for 0% -> 0%
where the time goes in v1:
time: 1840 us; the launch traced here: 1830 us
  waiting for transfers between devices  1320 us (72%)
  matrix products  211 us (11%)
  blocking collectives  169 us (9%)
  local copies, waits for them, and re-layouts  78 us (4%)
  other arithmetic  34.7 us (2%)
    reduce_scatter x1, waiting for transfers between devices, shards(): lax.psum_scatter(split_blocks(contract_rows(mixed, attended_grad), row_pa...  142 us
    reduce_scatter x1, waiting for transfers between devices, shards(): lax.psum_scatter(split_blocks(contract_rows(first_normed, query_base_grad...  141 us
    reduce_scatter x1, waiting for transfers between devices, shards(): lax.psum_scatter(down_grad, 'row', scatter_dimension=1, tiled=True)  124 us
    reduce_scatter x1, waiting for transfers between devices, shards(): lax.psum_scatter(up_grad, 'row', scatter_dimension=0, tiled=True)  124 us
    reduce_scatter x1, waiting for transfers between devices, shards(): lax.psum_scatter(split_blocks(contract_rows(first_normed, key_base_grad),...  104 us
    reduce_scatter x1, waiting for transfers between devices, shards(): lax.psum_scatter(split_blocks(contract_rows(first_normed, value_base_grad...  103 us
    reduce_scatter x1, waiting for transfers between devices, shards(): lax.psum_scatter(product(hidden, down_block), 'col', scatter_dimension=0,...  94 us
    unnamed x2, blocking collectives  86.9 us
  transfers between devices with their start and end apart: 23, of which 21 were waited for; matrix products, arithmetic and copies ran while one was open for 11% of the time, Pallas kernels for 0%

profile of v1, /device:TPU:0, one launch (start us, length us, event | category | flops | bytes accessed | tf_op | source)
XLA Modules:
  0.0 1829.8 jit_solution(9637498584656964820)
XLA Ops:
  11.6 42.2 %all-reduce.11 = (bf16[256]{0:T(256)(128)(2,1)S(1)}, bf16[1536]{0:T(1024)(128)(2,1)S(1)}, bf16[256]{0:T(256)(128)(2,1)S(1)}, bf16[1536]{0:T(1024)(128)(2,1)S(1)}, bf16[1536]{0:T(1024)(128)(2,1)S(1)}) all-reduce(bf16[256]{0:T(256)(128)(2,1)S(1)} %dynamic-update-slice.1, ...), channel_id=1, replica_groups=mesh['row'=4,'col'=8] {'row','col'}, use_global_device_ids=true, to_apply=%add.1 | all-reduce | flops 5120 | bytes 20480
  55.2 42.7 %all-gather = bf16[12288,32]{0,1:T(8,128)(2,1)S(1)} all-gather(bf16[384,32]{0,1:T(8,128)(2,1)} %param.23), channel_id=2, replica_groups=mesh['row'=4,'col'=8] {'row','col'}, dimensions={0}, use_global_device_ids=true | all-gather | bytes 811008 | tf_op jit(solution)/shard_map/all_gather | solution.py:128
  100.5 39.0 %all-gather.1 = bf16[12288,32]{0,1:T(8,128)(2,1)S(1)} all-gather(bf16[384,32]{0,1:T(8,128)(2,1)S(1)} %copy-done.36), channel_id=3, replica_groups=mesh['row'=4,'col'=8] {'row','col'}, dimensions={0}, use_global_device_ids=true | all-gather | bytes 811008 | tf_op jit(solution)/shard_map/all_gather | solution.py:127
  164.6 65.0 %all-gather.28.cloned.1.call-done = bf16[12288,192]{0,1:T(8,128)(2,1)} async-done(((bf16[384,192]{0,1:T(8,128)(2,1)}), bf16[12288,192]{0,1:T(8,128)(2,1)}) %all-gather.28.cloned.1.call-update) | async-done | bytes 4718608 | tf_op jit(solution)/shard_map/all_gather | solution.py:126
  243.6 50.6 %all-gather.30.cloned.1.call-done = bf16[12288,192]{0,1:T(8,128)(2,1)} async-done(((bf16[384,192]{0,1:T(8,128)(2,1)}), bf16[12288,192]{0,1:T(8,128)(2,1)}) %all-gather.30.cloned.1.call-update) | async-done | bytes 4718608 | tf_op jit(solution)/shard_map/all_gather | solution.py:129
  301.2 16.6 fusion.46
  337.8 24.1 %all-gather.20.cloned.1.call-done = bf16[1536,1120]{0,1:T(8,128)(2,1)} async-done(((bf16[384,1120]{0,1:T(8,128)(2,1)}), bf16[1536,1120]{0,1:T(8,128)(2,1)}) %all-gather.20.cloned.1.call-update) | async-done | bytes 3440656 | tf_op jit(solution)/shard_map/all_gather | solution.py:138
  361.9 46.3 %all-gather.18.cloned.1.call-done = bf16[2048,1536]{1,0:T(8,128)(2,1)} async-done(((bf16[256,1536]{1,0:T(8,128)(2,1)}), bf16[2048,1536]{1,0:T(8,128)(2,1)}) %all-gather.18.cloned.1.call-update) | async-done | bytes 6291472 | tf_op jit(solution)/shard_map/all_gather | solution.py:211
  421.2 56.7 %all-gather.22.cloned.1.call-done = bf16[1536,1120]{0,1:T(8,128)(2,1)} async-done(((bf16[384,1120]{0,1:T(8,128)(2,1)}), bf16[1536,1120]{0,1:T(8,128)(2,1)}) %all-gather.22.cloned.1.call-update) | async-done | bytes 3440656 | tf_op jit(solution)/shard_map/all_gather | solution.py:139
  490.8 55.4 %all-gather.26.cloned.1.call-done = bf16[1120,1536]{1,0:T(8,128)(2,1)} async-done(((bf16[1120,384]{1,0:T(8,128)(2,1)}), bf16[1120,1536]{1,0:T(8,128)(2,1)}) %all-gather.26.cloned.1.call-update) | async-done | bytes 3440656 | tf_op jit(solution)/shard_map/all_gather | solution.py:246
  546.2 45.9 %all-gather.24.cloned.1.call-done = bf16[2048,1536]{1,0:T(8,128)(2,1)} async-done(((bf16[256,1536]{1,0:T(8,128)(2,1)}), bf16[2048,1536]{1,0:T(8,128)(2,1)}) %all-gather.24.cloned.1.call-update) | async-done | bytes 6291472 | tf_op jit(solution)/shard_map/all_gather | solution.py:248
  592.1 20.8 %multiply_convert_fusion = (bf16[2048,1120]{0,1:T(8,128)(2,1)}, bf16[2048,1120]{0,1:T(8,128)(2,1)}, bf16[2048,1120]{0,1:T(8,128)(2,1)}) fusion(f32[2048,1120]{0,1:T(8,128)} %fusion.47, f32[2048,1120]{0,1:T(8,128)} %fusion.48, bf16[2048,1536]{1,0:T(8,128)(2,1)} %all-gather.24.cloned.1.call-done, bf16[1120,1536]{1,0:T(8,128)(2,1)} %all-gather.26.cloned.1.call-done), kind=kOutput, calls=%fused_computation.11 | convolution fusion | flops 7080837120 | bytes 41844736 | tf_op jit(solution)/shard_map/dot_general | solution.py:71
  642.9 21.6 %collective-permute-done = bf16[1120,384]{1,0:T(8,128)(2,1)S(1)} collective-permute-done((bf16[1120,384]{1,0:T(8,128)(2,1)S(1)}, bf16[1120,384]{1,0:T(8,128)(2,1)S(1)}, u32[]{:S(2)}, u32[]{:S(2)}) %collective-permute-start) | collective-permute-done | bytes 860192 | tf_op jit(solution)/shard_map/ppermute | solution.py:24
  665.4 22.3 %collective-permute-done.1 = bf16[1120,384]{1,0:T(8,128)(2,1)} collective-permute-done((bf16[1120,384]{1,0:T(8,128)(2,1)S(1)}, bf16[1120,384]{1,0:T(8,128)(2,1)}, u32[]{:S(2)}, u32[]{:S(2)}) %collective-permute-start.1) | collective-permute-done | bytes 860192 | tf_op jit(solution)/shard_map/ppermute | solution.py:24
  691.0 18.4 %collective-permute-done.2 = bf16[1120,384]{1,0:T(8,128)(2,1)} collective-permute-done((bf16[1120,384]{1,0:T(8,128)(2,1)}, bf16[1120,384]{1,0:T(8,128)(2,1)}, u32[]{:S(2)}, u32[]{:S(2)}) %collective-permute-start.2) | collective-permute-done | bytes 860192 | tf_op jit(solution)/shard_map/ppermute | solution.py:24
  734.6 94.0 %reduce-scatter.12.cloned.1.call-done = f32[256,1536]{1,0:T(8,128)} async-done(((f32[2048,1536]{1,0:T(8,128)}), f32[256,1536]{1,0:T(8,128)}) %reduce-scatter.12.cloned.1.call-update) | async-done | bytes 1572880 | tf_op jit(solution)/shard_map/reduce_scatter | solution.py:217
  993.0 44.6 %all-reduce.10 = (f32[1536]{0:T(1024)S(1)}, f32[1536]{0:T(1024)S(1)}, f32[256]{0:T(256)S(1)}, f32[256]{0:T(256)S(1)}, f32[1536]{0:T(1024)S(1)}) all-reduce(f32[1536]{0:T(1024)S(1)} %copy-done.35, f32[1536]{0:T(1024)S(1)} %bitcast.257, f32[256]{0:T(256)S(1)} %bitcast.261, ...), channel_id=10, replica_groups=mesh['row'=4,'col'=8] {'row','col'}, use_global_device_ids=true, to_apply=%region_15.16.clone | all-reduce | flops 5120 | bytes 40960
  1043.6 42.1 %reduce-scatter.28.cloned.1.call-done = f32[384,1120]{0,1:T(8,128)} async-done(((f32[1536,1120]{0,1:T(8,128)}), f32[384,1120]{0,1:T(8,128)}) %reduce-scatter.28.cloned.1.call-update) | async-done | bytes 1720336 | tf_op jit(solution)/shard_map/reduce_scatter | solution.py:361
  1085.7 123.6 %reduce-scatter.30.cloned.1.call-done = f32[384,1120]{0,1:T(8,128)} async-done(((f32[1536,1120]{0,1:T(8,128)}), f32[384,1120]{0,1:T(8,128)}) %reduce-scatter.30.cloned.1.call-update) | async-done | bytes 1720336 | tf_op jit(solution)/shard_map/reduce_scatter | solution.py:362
  1209.2 123.6 %reduce-scatter.32.cloned.1.call-done = f32[1120,384]{1,0:T(8,128)} async-done(((f32[1120,1536]{1,0:T(8,128)}), f32[1120,384]{1,0:T(8,128)}) %reduce-scatter.32.cloned.1.call-update) | async-done | bytes 1720336 | tf_op jit(solution)/shard_map/reduce_scatter | solution.py:363
  1332.9 104.1 %reduce-scatter.22.cloned.1.call-done = f32[1,384,32]{1,2,0:T(8,128)} async-done(((f32[32,384,32]{1,2,0:T(8,128)}), f32[1,384,32]{1,2,0:T(8,128)}) %reduce-scatter.22.cloned.1.call-update) | async-done | bytes 49168 | tf_op jit(solution)/shard_map/reduce_scatter | solution.py:331
  1437.0 102.6 %reduce-scatter.24.cloned.1.call-done = f32[1,384,32]{1,2,0:T(8,128)} async-done(((f32[32,384,32]{1,2,0:T(8,128)}), f32[1,384,32]{1,2,0:T(8,128)}) %reduce-scatter.24.cloned.1.call-update) | async-done | bytes 49168 | tf_op jit(solution)/shard_map/reduce_scatter | solution.py:337
  1539.6 141.7 %reduce-scatter.26.cloned.1.call-done = f32[1,384,192]{1,2,0:T(8,128)} async-done(((f32[32,384,192]{1,2,0:T(8,128)}), f32[1,384,192]{1,2,0:T(8,128)}) %reduce-scatter.26.cloned.1.call-update) | async-done | bytes 294928 | tf_op jit(solution)/shard_map/reduce_scatter | solution.py:343
  1681.3 141.4 %reduce-scatter.20.cloned.1.call-done = f32[1,384,192]{1,2,0:T(8,128)} async-done(((f32[32,384,192]{1,2,0:T(8,128)}), f32[1,384,192]{1,2,0:T(8,128)}) %reduce-scatter.20.cloned.1.call-update) | async-done | bytes 294928 | tf_op jit(solution)/shard_map/reduce_scatter | solution.py:325
  (265 shorter events, 329.0 us)
Async XLA Ops:
  7.2 138.5 %all-gather.14.cloned.1.call-start = ((), (), s32[]{:S(2)}) async-start(), calls=%async_computation.11 | async-start | bytes 1179648 | tf_op jit(solution)/shard_map/all_gather | solution.py:178
  53.8 181.9 %copy-start.32 = (f32[1536]{0:T(1024)}, f32[1536]{0:T(1024)S(1)}, u32[]{:S(2)}) copy-start(f32[1536]{0:T(1024)S(1)} %convert_element_type.134) | copy-start | bytes 18436
  100.5 62.8 %all-gather.16.cloned.1.call-start = ((), (), s32[]{:S(2)}) async-start(), calls=%async_computation.12 | async-start | bytes 1179648 | tf_op jit(solution)/shard_map/all_gather | solution.py:177
  142.3 87.4 %all-gather.28.cloned.1.call-start = ((), (), s32[]{:S(2)}) async-start(), calls=%async_computation.29 | async-start | bytes 4866048 | tf_op jit(solution)/shard_map/all_gather | solution.py:126
  143.0 151.2 %all-gather.30.cloned.1.call-start = ((), (), s32[]{:S(2)}) async-start(), calls=%async_computation.30 | async-start | bytes 4866048 | tf_op jit(solution)/shard_map/all_gather | solution.py:129
  143.6 218.3 %all-gather.20.cloned.1.call-start = ((), (), s32[]{:S(2)}) async-start(), calls=%async_computation.14 | async-start | bytes 4300800 | tf_op jit(solution)/shard_map/all_gather | solution.py:138
  144.2 264.0 %all-gather.18.cloned.1.call-start = ((), (), s32[]{:S(2)}) async-start(), calls=%async_computation.13 | async-start | bytes 7077888 | tf_op jit(solution)/shard_map/all_gather | solution.py:211
  335.5 142.4 %all-gather.22.cloned.1.call-start = ((), (), s32[]{:S(2)}) async-start(), calls=%async_computation.15 | async-start | bytes 4300800 | tf_op jit(solution)/shard_map/all_gather | solution.py:139
  336.3 209.9 %all-gather.26.cloned.1.call-start = ((), (), s32[]{:S(2)}) async-start(), calls=%async_computation.18 | async-start | bytes 4300800 | tf_op jit(solution)/shard_map/all_gather | solution.py:246
  337.0 255.0 %all-gather.24.cloned.1.call-start = ((), (), s32[]{:S(2)}) async-start(), calls=%async_computation.17 | async-start | bytes 7077888 | tf_op jit(solution)/shard_map/all_gather | solution.py:248
  337.7 395.0 %reduce-scatter.14.cloned.1.call-start = ((), (), s32[]{:S(2)}) async-start(), calls=%async_computation.19 | async-start | bytes 14155776 | tf_op jit(solution)/shard_map/reduce_scatter | solution.py:257
  640.3 188.3 %reduce-scatter.12.cloned.1.call-start = ((), (), s32[]{:S(2)}) async-start(), calls=%async_computation.16 | async-start | bytes 14155776 | tf_op jit(solution)/shard_map/reduce_scatter | solution.py:217
  641.4 23.1 %collective-permute-start = (bf16[1120,384]{1,0:T(8,128)(2,1)S(1)}, bf16[1120,384]{1,0:T(8,128)(2,1)S(1)}, u32[]{:S(2)}, u32[]{:S(2)}) collective-permute-start(bf16[1120,384]{1,0:T(8,128)(2,1)S(1)} %copy-done.12), channel_id=1, source_target_pairs={{0,8},{8,16},{16,24},{24,0},{1,9},{9,17},{17,25},{25,1},{2,10},{10... | collective-permute-start | bytes 2580488 | tf_op jit(solution)/shard_map/ppermute | solution.py:24
  665.4 22.3 %collective-permute-start.1 = (bf16[1120,384]{1,0:T(8,128)(2,1)S(1)}, bf16[1120,384]{1,0:T(8,128)(2,1)}, u32[]{:S(2)}, u32[]{:S(2)}) collective-permute-start(bf16[1120,384]{1,0:T(8,128)(2,1)S(1)} %collective-permute-done), channel_id=1, source_target_pairs={{0,8},{8,16},{16,24},{24,0},{1,9},{9,17},{17,25},{25,1},{2,10},{10... | collective-permute-start | bytes 2580488 | tf_op jit(solution)/shard_map/ppermute | solution.py:24
  687.7 21.7 %collective-permute-start.2 = (bf16[1120,384]{1,0:T(8,128)(2,1)}, bf16[1120,384]{1,0:T(8,128)(2,1)}, u32[]{:S(2)}, u32[]{:S(2)}) collective-permute-start(bf16[1120,384]{1,0:T(8,128)(2,1)} %collective-permute-done.1), channel_id=1, source_target_pairs={{0,8},{8,16},{16,24},{24,0},{1,9},{9,17},{17,25},{25,1},{2,10},{10... | collective-permute-start | bytes 2580488 | tf_op jit(solution)/shard_map/ppermute | solution.py:24
  722.0 225.2 %reduce-scatter.16.cloned.1.call-start = ((), (), s32[]{:S(2)}) async-start(), calls=%async_computation.20 | async-start | bytes 2359296 | tf_op jit(solution)/shard_map/reduce_scatter | solution.py:298
  875.8 85.7 %reduce-scatter.18.cloned.1.call-start = ((), (), s32[]{:S(2)}) async-start(), calls=%async_computation.21 | async-start | bytes 2359296 | tf_op jit(solution)/shard_map/reduce_scatter | solution.py:299
  895.3 190.4 %reduce-scatter.28.cloned.1.call-start = ((), (), s32[]{:S(2)}) async-start(), calls=%async_computation.26 | async-start | bytes 8601600 | tf_op jit(solution)/shard_map/reduce_scatter | solution.py:361
  908.3 300.9 %reduce-scatter.30.cloned.1.call-start = ((), (), s32[]{:S(2)}) async-start(), calls=%async_computation.27 | async-start | bytes 8601600 | tf_op jit(solution)/shard_map/reduce_scatter | solution.py:362
  921.3 411.5 %reduce-scatter.32.cloned.1.call-start = ((), (), s32[]{:S(2)}) async-start(), calls=%async_computation.28 | async-start | bytes 8601600 | tf_op jit(solution)/shard_map/reduce_scatter | solution.py:363
  934.0 502.9 %reduce-scatter.22.cloned.1.call-start = ((), (), s32[]{:S(2)}) async-start(), calls=%async_computation.23 | async-start | bytes 1622016 | tf_op jit(solution)/shard_map/reduce_scatter | solution.py:331
  968.8 570.8 %reduce-scatter.24.cloned.1.call-start = ((), (), s32[]{:S(2)}) async-start(), calls=%async_computation.24 | async-start | bytes 1622016 | tf_op jit(solution)/shard_map/reduce_scatter | solution.py:337
  977.0 704.3 %reduce-scatter.26.cloned.1.call-start = ((), (), s32[]{:S(2)}) async-start(), calls=%async_computation.25 | async-start | bytes 9732096 | tf_op jit(solution)/shard_map/reduce_scatter | solution.py:343
  986.1 836.7 %reduce-scatter.20.cloned.1.call-start = ((), (), s32[]{:S(2)}) async-start(), calls=%async_computation.22 | async-start | bytes 9732096 | tf_op jit(solution)/shard_map/reduce_scatter | solution.py:325
  (50 other events, 1114.7 us)
Sparse Core Ops, SparseCore 0:
  100.6 21.2 all-gather.13
  142.4 20.8 all-gather.15
  166.0 63.5 all-gather.27
  232.3 61.8 all-gather.29
  295.6 66.2 all-gather.19
  364.2 43.9 all-gather.17
  409.8 68.0 all-gather.21
  479.5 66.6 all-gather.25
  548.1 43.9 all-gather.23
  640.4 92.2 reduce-scatter.13
  736.2 92.2 reduce-scatter.11
  875.9 41.1 reduce-scatter.15
  920.3 41.1 reduce-scatter.17
  964.2 121.3 reduce-scatter.27
  1088.4 120.7 reduce-scatter.29
  1212.0 120.8 reduce-scatter.31
  1338.5 98.3 reduce-scatter.21
  1442.6 96.9 reduce-scatter.23
  1546.1 135.1 reduce-scatter.25
  1687.6 135.0 reduce-scatter.19
